TPU v7x, 32 devices: a whole 2x2x4 slice. The times are simulated.
32 devices in a mesh: rows: 8 (over z, y), protos: 4 (over x, core).
Axes of the slice: x: 2, y: 2, z: 4, core: 2. Of those that a mesh axis runs over, the one named last changes fastest.
Arguments:
- features: bfloat16 [3072, 256], P('rows', 'protos'), may hold values from -12 to 12
- prototypes: bfloat16 [65536, 256], P('protos', 'rows'), may hold values from -8 to 8
- masked_index: int32 [1536], P('rows'), may hold values from 0 to 383
Outputs:
- targets: bfloat16 [1536, 65536], P('rows', 'protos')
Inputs may be any that keep to these rules, and one draw needn't show every extreme that they name: Row r of the whole takes patch (r // 192) * 384 + masked_index[r] of features.
All inputs are finite; a program needn't handle non-finite values.
Results may differ from a plain program's by a relative error of at most 0.001.
Values may be sent and summed in bfloat16 or wider, within the bound.
A program may use at most 64 MiB of HBM per device.

v0:
```python
import jax
import jax.numpy as jnp
from jax import lax
from jax.sharding import PartitionSpec as P

K = 65536
ITERS = 3


TEMP = 0.07
EPS = 1e-06


def on_device(features, prototypes, masked_index):
    chosen = jnp.take(features, masked_index, axis=0)
    patches = lax.all_gather(chosen, "protos", axis=1, tiled=True)
    feat_scale = lax.rsqrt(jnp.sum(jnp.square(patches.astype(jnp.float32)), axis=1) + EPS)
    full = lax.all_gather(prototypes, "rows", axis=1, tiled=True)
    proto_sq = jnp.sum(jnp.square(full.astype(jnp.float32)), axis=1)
    raw = lax.dot_general(
        patches, full, (((1,), (1,)), ((), ())), preferred_element_type=jnp.float32
    )
    proto_scale = lax.rsqrt(proto_sq + EPS)
    weights = jnp.exp(raw * feat_scale[:, None] * proto_scale[None, :] / TEMP)
    total_rows = masked_index.shape[0] * lax.axis_size("rows")
    row_scale = jnp.ones((patches.shape[0],), jnp.float32)
    for step in range(ITERS):
        col_part = jnp.dot(row_scale, weights, precision=lax.Precision.HIGHEST)
        col_scale = 1.0 / (K * lax.psum(col_part, "rows"))
        row_part = jnp.dot(weights, col_scale, precision=lax.Precision.HIGHEST)
        row_scale = 1.0 / (total_rows * lax.psum(row_part, "protos"))
    factor = float(K) * float(total_rows)
    return (factor * row_scale[:, None] * weights * col_scale[None, :]).astype(jnp.bfloat16)


def solution(mesh):
    in_specs = (P("rows", "protos"), P("protos", "rows"), P("rows"))
    out_specs = P("rows", "protos")
    return jax.shard_map(
        on_device, mesh=mesh, in_specs=in_specs, out_specs=out_specs, check_vma=False
    )
```

profile of v0, /device:TPU:0, one launch (start us, length us, event | category | flops | bytes accessed | tf_op | source)
XLA Modules:
  0.0 458.1 jit_solution(18258766225013638009)
XLA Ops:
  6.5 0.7 all-gather.2.cloned.1.call-update
  7.3 0.9 copy.5
  8.9 0.8 gather_fusion
  10.6 6.5 %all_gather.6 = bf16[192,256]{0,1:T(8,128)(2,1)S(1)} all-gather(bf16[192,64]{0,1:T(8,128)(2,1)S(1)} %copy.6), channel_id=1, replica_groups=mesh['rows'=8,'protos'=4] {'protos'}, dimensions={1}, use_global_device_ids=true | all-gather | bytes 122880 | tf_op jit(solution)/shard_map/all_gather | solution.py:16
  17.2 119.5 %all-gather.2.cloned.1.call-done = bf16[16384,256]{0,1:T(8,128)(2,1)} async-done(((bf16[16384,32]{0,1:T(8,128)(2,1)}), bf16[16384,256]{0,1:T(8,128)(2,1)}) %all-gather.2.cloned.1.call-update) | async-done | bytes 8388624 | tf_op jit(solution)/shard_map/all_gather | solution.py:18
  136.7 5.1 %multiply_reduce_fusion = f32[16384]{0:T(1024)S(1)} fusion(bf16[16384,256]{0,1:T(8,128)(2,1)} %all-gather.2.cloned.1.call-done), kind=kLoop, calls=%fused_computation.5 | loop fusion | flops 12566528 | bytes 8454144 | tf_op jit(solution)/shard_map/reduce_sum | solution.py:19
  141.8 5.8 %fusion.2 = f32[192,16384]{1,0:T(8,128)S(1)} fusion(bf16[192,256]{0,1:T(8,128)(2,1)S(1)} %all_gather.6, bf16[16384,256]{0,1:T(8,128)(2,1)} %all-gather.2.cloned.1.call-done, f32[16384]{0:T(1024)S(1)} %add_rsqrt_fusion, f32[192]{0:T(256)S(1)} %add_rsqrt_fusion.1), kind=kOutput, calls=%fused_computation.4 | convolution fusion | flops 1620049920 | bytes 21136128 | tf_op jit(solution)/shard_map/dot_general | solution.py:20
  147.7 4.6 copy-done
  152.2 6.6 %fusion.3 = f32[1,16384]{1,0:T(1,128)} fusion(f32[192,16384]{1,0:T(8,128)S(1)} %fusion.2), kind=kOutput, calls=%fused_computation.20 | convolution fusion | flops 37748736 | bytes 12648448 | tf_op jit(solution)/shard_map/dot_general | solution.py:28
  159.1 67.3 %all-reduce.4.cloned.1.call-done = f32[16384]{0:T(1024)} async-done(((f32[16384]{0:T(1024)}), f32[16384]{0:T(1024)}) %all-reduce.4.cloned.1.call-update) | async-done | bytes 65552 | tf_op jit(solution)/shard_map/psum | solution.py:29
  226.4 0.9 multiply_divide_fusion.2
  227.3 12.7 %fusion.6 = f32[1,192]{1,0:T(1,128)S(1)} fusion(f32[192,16384]{1,0:T(8,128)} %copy-done, f32[16384,1]{0,1:T(1,128)S(1)} %bitcast.28), kind=kOutput, calls=%fused_computation.23 | convolution fusion | flops 37748736 | bytes 12649216 | tf_op jit(solution)/shard_map/dot_general | solution.py:30
  240.0 5.7 %psum.43 = f32[192]{0:T(256)S(1)} all-reduce(f32[192]{0:T(256)S(1)} %bitcast.30), channel_id=1, replica_groups=mesh['rows'=8,'protos'=4] {'protos'}, use_global_device_ids=true, to_apply=%region_3.4 | all-reduce | flops 192 | bytes 1536 | tf_op jit(solution)/shard_map/psum | solution.py:31
  245.7 9.5 %fusion.7 = f32[1,16384]{1,0:T(1,128)} fusion(f32[192,1]{0,1:T(1,128)S(1)} %bitcast.31, f32[192,16384]{1,0:T(8,128)} %copy-done), kind=kOutput, calls=%fused_computation.24 | convolution fusion | flops 37748736 | bytes 12649216 | tf_op jit(solution)/shard_map/dot_general | solution.py:28
  255.3 69.6 %all-reduce.6.cloned.1.call-done = f32[16384]{0:T(1024)} async-done(((f32[16384]{0:T(1024)}), f32[16384]{0:T(1024)}) %all-reduce.6.cloned.1.call-update) | async-done | bytes 65552 | tf_op jit(solution)/shard_map/psum | solution.py:29
  324.8 0.9 multiply_divide_fusion.1
  325.7 12.7 %fusion.8 = f32[1,192]{1,0:T(1,128)S(1)} fusion(f32[192,16384]{1,0:T(8,128)} %copy-done, f32[16384,1]{0,1:T(1,128)S(1)} %bitcast.29), kind=kOutput, calls=%fused_computation.25 | convolution fusion | flops 37748736 | bytes 12649216 | tf_op jit(solution)/shard_map/dot_general | solution.py:30
  338.4 5.9 %psum.45 = f32[192]{0:T(256)S(1)} all-reduce(f32[192]{0:T(256)S(1)} %bitcast.32), channel_id=1, replica_groups=mesh['rows'=8,'protos'=4] {'protos'}, use_global_device_ids=true, to_apply=%region_5.6 | all-reduce | flops 192 | bytes 1536 | tf_op jit(solution)/shard_map/psum | solution.py:31
  344.3 9.5 %fusion.9 = f32[1,16384]{1,0:T(1,128)} fusion(f32[192,1]{0,1:T(1,128)S(1)} %bitcast.33, f32[192,16384]{1,0:T(8,128)} %copy-done), kind=kOutput, calls=%fused_computation.26 | convolution fusion | flops 37748736 | bytes 12649216 | tf_op jit(solution)/shard_map/dot_general | solution.py:28
  353.8 69.6 %all-reduce.8.cloned.1.call-done = f32[16384]{0:T(1024)} async-done(((f32[16384]{0:T(1024)}), f32[16384]{0:T(1024)}) %all-reduce.8.cloned.1.call-update) | async-done | bytes 65552 | tf_op jit(solution)/shard_map/psum | solution.py:29
  423.5 0.9 multiply_divide_fusion
  424.3 12.7 %fusion.10 = f32[1,192]{1,0:T(1,128)S(1)} fusion(f32[192,16384]{1,0:T(8,128)} %copy-done, f32[16384,1]{0,1:T(1,128)S(1)} %bitcast.24), kind=kOutput, calls=%fused_computation.27 | convolution fusion | flops 37748736 | bytes 12649216 | tf_op jit(solution)/shard_map/dot_general | solution.py:30
  437.0 5.7 %psum.47 = f32[192]{0:T(256)S(1)} all-reduce(f32[192]{0:T(256)S(1)} %bitcast.34), channel_id=1, replica_groups=mesh['rows'=8,'protos'=4] {'protos'}, use_global_device_ids=true, to_apply=%region_7.8 | all-reduce | flops 192 | bytes 1536 | tf_op jit(solution)/shard_map/psum | solution.py:31
  442.7 8.8 %multiply_convert_fusion = bf16[192,16384]{1,0:T(8,128)(2,1)} fusion(f32[192,16384]{1,0:T(8,128)} %copy-done, f32[16384]{0:T(1024)S(1)} %multiply_divide_fusion, f32[192]{0:T(256)S(1)} %divide_multiply_fusion), kind=kLoop, calls=%fused_computation.6 | loop fusion | flops 9437184 | bytes 18940672 | tf_op jit(solution)/shard_map/convert_element_type | solution.py:33
  (19 shorter events, 2.0 us)
Async XLA Ops:
  6.5 130.2 %all-gather.2.cloned.1.call-start = ((), (), s32[]{:S(2)}) async-start(), calls=%async_computation | async-start | bytes 9437184 | tf_op jit(solution)/shard_map/all_gather | solution.py:18
  7.3 219.2 %all-reduce.4.cloned.1.call-start = ((), (), s32[]{:S(2)}) async-start(), calls=%async_computation.1 | async-start | bytes 131072 | tf_op jit(solution)/shard_map/psum | solution.py:29
  147.7 4.6 copy-start
  158.9 166.0 %all-reduce.6.cloned.1.call-start = ((), (), s32[]{:S(2)}) async-start(), calls=%async_computation.2 | async-start | bytes 131072 | tf_op jit(solution)/shard_map/psum | solution.py:29
  255.2 168.3 %all-reduce.8.cloned.1.call-start = ((), (), s32[]{:S(2)}) async-start(), calls=%async_computation.3 | async-start | bytes 131072 | tf_op jit(solution)/shard_map/psum | solution.py:29
Sparse Core Ops, SparseCore 0:
  9.5 127.1 all-gather.1
  159.0 67.3 all-reduce.3
  255.3 69.4 all-reduce.5
  354.0 69.4 all-reduce.7
where the time goes:
time: 459 us; the launch traced here: 458 us
  waiting for transfers between devices  327 us (71%)
  matrix products  69.6 us (15%)
  blocking collectives  23.7 us (5%)
  other arithmetic  18.1 us (4%)
  between operations  13.2 us (3%)
  local copies, waits for them, and re-layouts  6.35 us (1%)
    psum x3, waiting for transfers between devices, on_device(): col_scale = 1.0 / (K * lax.psum(col_part, 'rows'))  207 us
    all_gather x1, waiting for transfers between devices, on_device(): full = lax.all_gather(prototypes, 'rows', axis=1, tiled=True)  120 us
    dot_general x3, matrix products, on_device(): row_part = jnp.dot(weights, col_scale, precision=lax.Precision.HIGHEST)  38.2 us
    dot_general x3, matrix products, on_device(): col_part = jnp.dot(row_scale, weights, precision=lax.Precision.HIGHEST)  25.6 us
    psum x3, blocking collectives, on_device(): row_scale = 1.0 / (total_rows * lax.psum(row_part, 'protos'))  17.2 us
  transfers between devices with their start and end apart: 4, of which 4 were waited for; matrix products, arithmetic and copies ran while one was open for 1% of the time, Pallas kernels for 0%

commit v1 on v0

v1 whole, which is shorter than its diff:
```python
import functools

import jax
import jax.numpy as jnp
from jax import lax
from jax.experimental import pallas as pl
from jax.experimental.pallas import tpu as pltpu
from jax.sharding import PartitionSpec as P

ITERS = 3


TEMP = 0.07
EPS = 1e-06
UP, DOWN, ACROSS = 0, 1, 2
LEAD = 2


def kernel(
    n_rows, n_protos, masked, protos_all,
    feat_ref, proto_ref, index_ref, weights_ref, rs_ref, cs_ref,
    feat_full, full, chosen, feat_scale, weights, acc, parts, masses, row_out, row_in,
    feat_send, feat_recv, own_sem, send, recv, out_sem,
    mass_send, mass_recv, scale_send, scale_recv, row_send, row_recv,
):
    r, p = lax.axis_index("rows"), lax.axis_index("protos")
    z, y = r // 2, lax.rem(r, 2)
    nz = n_rows // 2
    other = 1 - y
    dim, total = proto_ref.shape
    width = total // n_rows
    rows = index_ref.shape[0]
    fdim = feat_ref.shape[0]
    tile = min(512, width)
    tiles = width // tile
    mesh_id = pl.DeviceIdType.MESH

    barrier = pltpu.get_barrier_semaphore()
    for step in range(1, n_rows):
        pl.semaphore_signal(
            barrier, inc=1, device_id={"rows": lax.rem(r + step, n_rows)}, device_id_type=mesh_id
        )
    for step in range(1, n_protos):
        pl.semaphore_signal(
            barrier, inc=1, device_id={"protos": lax.rem(p + step, n_protos)}, device_id_type=mesh_id
        )
    pl.semaphore_wait(barrier, n_rows + n_protos - 2)

    def where(src, c):
        return (
            pl.ds(pl.multiple_of(src * dim, dim), dim),
            pl.ds(pl.multiple_of(c * width, width), width),
        )

    def block_copy(way, src, c, own=False):
        spot = where(src, c)
        target = {UP: r + 2, DOWN: r - 2, ACROSS: z * 2 + other}[way]
        return pltpu.make_async_remote_copy(
            src_ref=proto_ref.at[:, spot[1]] if own else full.at[spot],
            dst_ref=full.at[spot],
            send_sem=send.at[way, src, c],
            recv_sem=recv.at[src, c],
            device_id={"rows": target},
            device_id_type=mesh_id,
        )

    def own_copy(c):
        return pltpu.make_async_copy(
            proto_ref.at[:, where(r, c)[1]], full.at[where(r, c)], own_sem.at[c]
        )

    def send_own(c):
        @pl.when(z < nz - 1)
        def _():
            block_copy(UP, r, c, True).start()

        @pl.when(z > 0)
        def _():
            block_copy(DOWN, r, c, True).start()

        block_copy(ACROSS, r, c, True).start()
        own_copy(c).start()

    def feat_copy(step):
        block = pl.ds(pl.multiple_of(p * fdim, fdim), fdim)
        return pltpu.make_async_remote_copy(
            src_ref=feat_ref,
            dst_ref=feat_full.at[block],
            send_sem=feat_send.at[step],
            recv_sem=feat_recv.at[step],
            device_id={"protos": lax.rem(p + step, n_protos)},
            device_id_type=mesh_id,
        )

    for step in range(1, n_protos):
        feat_copy(step).start()
    for c in range(LEAD):
        send_own(c)
    feat_full[pl.ds(pl.multiple_of(p * fdim, fdim), fdim), :] = feat_ref[...]
    for step in range(1, n_protos):
        feat_copy(step).wait()
    onehot = lax.broadcasted_iota(jnp.int32, (rows, feat_ref.shape[1]), 1) == index_ref[...]
    picked = lax.dot_general(
        onehot.astype(jnp.float32).astype(jnp.bfloat16),
        feat_full[...],
        (((1,), (1,)), ((), ())),
        preferred_element_type=jnp.float32,
    )
    chosen[...] = picked.astype(jnp.bfloat16)
    scale = lax.rsqrt(jnp.sum(picked * picked, axis=1, keepdims=True) + EPS)
    feat_scale[...] = jnp.broadcast_to(scale * (1.0 / TEMP), feat_scale.shape)
    acc[...] = jnp.zeros_like(acc)

    def mass_copy(it, c, sender):
        return pltpu.make_async_remote_copy(
            src_ref=parts.at[it, c],
            dst_ref=masses.at[it, sender],
            send_sem=mass_send.at[it, c],
            recv_sem=mass_recv.at[it, sender],
            device_id={"rows": c},
            device_id_type=mesh_id,
        )

    def give_mass(it, c):
        @pl.when(c == r)
        def _():
            masses[it, c] = parts[it, c]

        @pl.when(c != r)
        def _():
            mass_copy(it, c, r).start()

    def out_copy(c):
        columns = where(r, c)[1]
        return pltpu.make_async_copy(
            weights.at[:, columns], weights_ref.at[:, columns], out_sem.at[c]
        )

    def make_weights(c):
        for t in range(tiles):
            columns = pl.ds(pl.multiple_of(c * width + t * tile, tile), tile)
            block = full[:, columns]
            wide = block.astype(jnp.float32)
            proto_scale = lax.rsqrt(jnp.sum(wide * wide, axis=0, keepdims=True) + EPS)
            raw = jnp.dot(chosen[...], block, preferred_element_type=jnp.float32)
            value = jnp.exp(raw * feat_scale[:, :1] * proto_scale)
            weights[:, columns] = value
            parts[0, c, :, t * tile:(t + 1) * tile] = jnp.sum(value, axis=0, keepdims=True)

    middle = n_rows // 2

    def line(c, d):
        for way, ahead, more, there in (
            (DOWN, z + d, z > 0, z + d < nz),
            (UP, z - d, z < nz - 1, z - d >= 0),
        ):
            src = ahead * 2 + y

            @pl.when(there)
            def _():
                block_copy(ACROSS, src, c).wait_recv()

                @pl.when(more)
                def _():
                    block_copy(way, src, c).start()

                @pl.when(c != middle)
                def _():
                    block_copy(ACROSS, src, c).start()

    def far_line(c, d):
        for way, ahead, more, there in (
            (DOWN, z + d, z > 0, z + d < nz),
            (UP, z - d, z < nz - 1, z - d >= 0),
        ):
            src = ahead * 2 + other

            @pl.when(there)
            def _():
                block_copy(ACROSS, src, c).wait_recv()

                @pl.when(jnp.logical_and(more, c == middle))
                def _():
                    block_copy(way, src, c).start()

    def beside(c):
        src = z * 2 + other
        block_copy(ACROSS, src, c).wait_recv()

        @pl.when(jnp.logical_and(z < nz - 1, c == middle))
        def _():
            block_copy(UP, src, c).start()

        @pl.when(jnp.logical_and(z > 0, c == middle))
        def _():
            block_copy(DOWN, src, c).start()

    def step_of(i, carry):
        @pl.when(i + LEAD < n_rows)
        def _():
            send_own(i + LEAD)

        @pl.when(i < n_rows)
        def _():
            beside(i)

        for d in range(1, nz):
            c = i - (d - 1)

            @pl.when(jnp.logical_and(c >= 0, c < n_rows))
            def _():
                line(c, d)

        last = i - (nz - 1)

        @pl.when(last >= 0)
        def _():
            for d in range(1, nz):
                far_line(last, d)
            own_copy(last).wait()
            make_weights(last)
            out_copy(last).start()
            give_mass(0, last)

        return carry

    lax.fori_loop(0, n_rows + nz - 1, step_of, 0)

    def scale_copy(it, c, step):
        return pltpu.make_async_remote_copy(
            src_ref=cs_ref.at[it, c],
            dst_ref=cs_ref.at[it, c],
            send_sem=scale_send.at[it, step],
            recv_sem=scale_recv.at[it, c],
            device_id={"rows": lax.rem(r + step, n_rows)},
            device_id_type=mesh_id,
        )

    def row_copy(it, step):
        return pltpu.make_async_remote_copy(
            src_ref=row_out.at[it],
            dst_ref=row_in.at[it, step],
            send_sem=row_send.at[it, step],
            recv_sem=row_recv.at[it, step],
            device_id={"protos": lax.rem(p + step, n_protos)},
            device_id_type=mesh_id,
        )

    for it in range(ITERS):
        if it > 0:
            row_scale = rs_ref[:rows, :1]

            def col_pass(j, carry):
                c = lax.rem(r + 1 + j, n_rows)
                for t in range(tiles):
                    columns = pl.ds(pl.multiple_of(c * width + t * tile, tile), tile)
                    value = jnp.sum(weights[:, columns] * rs_ref[:rows, :1], axis=0, keepdims=True)
                    parts[it, c, :, t * tile:(t + 1) * tile] = value
                give_mass(it, c)
                return carry

            lax.fori_loop(0, n_rows, col_pass, 0)
        for step in range(1, n_rows):
            mass_copy(it, r, lax.rem(r + step, n_rows)).wait_recv()
        cs_ref[it, r] = 1.0 / (protos_all * jnp.sum(masses[it], axis=0))
        for step in range(1, n_rows):
            scale_copy(it, r, step).start()

        def row_pass(j, total):
            c = lax.rem(r + j, n_rows)

            @pl.when(j > 0)
            def _():
                scale_copy(it, c, 1).wait_recv()

            for t in range(width // 128):
                columns = pl.ds(pl.multiple_of(c * width + t * 128, 128), 128)
                total = total + weights[:, columns] * cs_ref[it, c, :, t * 128:(t + 1) * 128]
            return total

        summed = lax.fori_loop(0, n_rows, row_pass, jnp.zeros((rows, 128), jnp.float32))
        acc[:rows, :] = summed
        row_out[it] = jnp.sum(acc[...].T, axis=0, keepdims=True)
        for step in range(1, n_protos):
            row_copy(it, step).start()
        mass = row_out[it]
        for step in range(1, n_protos):
            row_copy(it, step).wait_recv()
            mass = mass + row_in[it, step]
        turned = jnp.broadcast_to(1.0 / (masked * mass), (128, acc.shape[0])).T
        rs_ref[...] = turned

    for it in range(ITERS):
        for step in range(1, n_rows):
            mass_copy(it, lax.rem(r + step, n_rows), r).wait_send()
            scale_copy(it, r, step).wait_send()
        for step in range(1, n_protos):
            row_copy(it, step).wait_send()

    def drain(c, carry):
        out_copy(c).wait()
        for src_z in range(nz):
            for src_y in range(2):
                src = src_z * 2 + src_y
                on_line = src_y == y
                beside_me = jnp.logical_and(src_y != y, src_z == z)
                moved = jnp.logical_or(on_line, c == middle)

                @pl.when(jnp.logical_and(moved, jnp.logical_and(src_z <= z, z < nz - 1)))
                def _():
                    block_copy(UP, src, c).wait_send()

                @pl.when(jnp.logical_and(moved, jnp.logical_and(src_z >= z, z > 0)))
                def _():
                    block_copy(DOWN, src, c).wait_send()

                @pl.when(jnp.logical_and(on_line, jnp.logical_or(src_z == z, c != middle)))
                def _():
                    block_copy(ACROSS, src, c).wait_send()

        return carry

    lax.fori_loop(0, n_rows, drain, 0)


def with_kernel(n_rows, n_protos, features, prototypes, masked_index):
    rows = masked_index.shape[0]
    dim, total = prototypes.shape[1], prototypes.shape[0]
    fdim, patches = features.shape[1], features.shape[0]
    width = total // n_rows
    padded = -(-rows // 128) * 128
    masked = float(rows * n_rows)
    protos_all = float(total * n_protos)
    f32, bf16, dma = jnp.float32, jnp.bfloat16, pltpu.SemaphoreType.DMA
    vmem = pl.BlockSpec(memory_space=pltpu.VMEM)
    anywhere = pl.BlockSpec(memory_space=pl.ANY)
    weights, rs, cs = pl.pallas_call(
        functools.partial(kernel, n_rows, n_protos, masked, protos_all),
        out_shape=(
            jax.ShapeDtypeStruct((rows, total), f32),
            jax.ShapeDtypeStruct((padded, 128), f32),
            jax.ShapeDtypeStruct((ITERS, n_rows, 1, width), f32),
        ),
        in_specs=[vmem, anywhere, vmem],
        out_specs=(anywhere, vmem, vmem),
        scratch_shapes=[
            pltpu.VMEM((fdim * n_protos, patches), bf16),
            pltpu.VMEM((dim * n_rows, total), bf16),
            pltpu.VMEM((rows, fdim * n_protos), bf16),
            pltpu.VMEM((rows, 128), f32),
            pltpu.VMEM((rows, total), f32),
            pltpu.VMEM((padded, 128), f32),
            pltpu.VMEM((ITERS, n_rows, 1, width), f32),
            pltpu.VMEM((ITERS, n_rows, 1, width), f32),
            pltpu.VMEM((ITERS, 1, padded), f32),
            pltpu.VMEM((ITERS, n_protos, 1, padded), f32),
            dma((n_protos,)),
            dma((n_protos,)),
            dma((n_rows,)),
            dma((3, n_rows, n_rows)),
            dma((n_rows, n_rows)),
            dma((n_rows,)),
            dma((ITERS, n_rows)),
            dma((ITERS, n_rows)),
            dma((ITERS, n_rows)),
            dma((ITERS, n_rows)),
            dma((ITERS, n_protos)),
            dma((ITERS, n_protos)),
        ],
        compiler_params=pltpu.CompilerParams(
            collective_id=0, has_side_effects=True, vmem_limit_bytes=48 * 1024 * 1024
        ),
    )(features.T, prototypes.T, masked_index[:, None])
    row_scale = (protos_all * masked) * rs[:rows, :1]
    return (row_scale * weights * cs[ITERS - 1].reshape(1, total)).astype(jnp.bfloat16)


def with_collectives(features, prototypes, masked_index):
    total_protos = float(prototypes.shape[0] * lax.axis_size("protos"))
    chosen = jnp.take(features, masked_index, axis=0)
    patches = lax.all_gather(chosen, "protos", axis=1, tiled=True)
    feat_scale = lax.rsqrt(jnp.sum(jnp.square(patches.astype(jnp.float32)), axis=1) + EPS)
    full = lax.all_gather(prototypes, "rows", axis=1, tiled=True)
    proto_sq = jnp.sum(jnp.square(full.astype(jnp.float32)), axis=1)
    raw = lax.dot_general(
        patches, full, (((1,), (1,)), ((), ())), preferred_element_type=jnp.float32
    )
    proto_scale = lax.rsqrt(proto_sq + EPS)
    weights = jnp.exp(raw * feat_scale[:, None] * proto_scale[None, :] / TEMP)
    total_rows = masked_index.shape[0] * lax.axis_size("rows")
    row_scale = jnp.ones((patches.shape[0],), jnp.float32)
    for step in range(ITERS):
        col_part = jnp.dot(row_scale, weights, precision=lax.Precision.HIGHEST)
        col_scale = 1.0 / (total_protos * lax.psum(col_part, "rows"))
        row_part = jnp.dot(weights, col_scale, precision=lax.Precision.HIGHEST)
        row_scale = 1.0 / (total_rows * lax.psum(row_part, "protos"))
    factor = total_protos * float(total_rows)
    return (factor * row_scale[:, None] * weights * col_scale[None, :]).astype(jnp.bfloat16)


def solution(mesh):
    n_rows, n_protos = mesh.shape["rows"], mesh.shape["protos"]
    in_specs = (P("rows", "protos"), P("protos", "rows"), P("rows"))
    out_specs = P("rows", "protos")

    def on_device(features, prototypes, masked_index):
        fits = (
            n_rows % 2 == 0
            and n_rows <= 8
            and prototypes.shape[1] % 16 == 0
            and features.shape[1] % 16 == 0
            and prototypes.shape[0] % (n_rows * 128) == 0
        )
        if fits:
            return with_kernel(n_rows, n_protos, features, prototypes, masked_index)
        return with_collectives(features, prototypes, masked_index)

    return jax.shard_map(
        on_device, mesh=mesh, in_specs=in_specs, out_specs=out_specs, check_vma=False
    )
```

time: 459 us -> 144 us (0.31)
  waiting for transfers between devices: 327 us -> 0 us
  Pallas kernels: 0 us -> 132 us
  matrix products: 69.6 us -> 0 us
  blocking collectives: 23.7 us -> 0 us
  between operations: 13.2 us -> 0.04 us
  other arithmetic: 18.1 us -> 8.94 us
    psum x3 -> x0, waiting for transfers between devices: 207 us -> none  [on_device(): col_scale = 1.0 / (K * lax.psum(col_part, 'rows'))]
    pallas_call x0 -> x1, Pallas kernels: none -> 132 us  [with_kernel(): pl.pallas_call(functools.partial(kernel, n_rows, n_protos, masked, protos...]
    all_gather x1 -> x0, waiting for transfers between devices: 120 us -> none  [on_device(): full = lax.all_gather(prototypes, 'rows', axis=1, tiled=True)]
    dot_general x7 -> x0, matrix products: 69.6 us -> none  [the longest x3 38.2 us: on_device(): row_part = jnp.dot(weights, col_scale, precision=lax.Precision.HIGHEST)]
    psum x3 -> x0, blocking collectives: 17.2 us -> none  [on_device(): row_scale = 1.0 / (total_rows * lax.psum(row_part, 'protos'))]
    all_gather x1 -> x0, blocking collectives: 6.51 us -> none  [on_device(): patches = lax.all_gather(chosen, 'protos', axis=1, tiled=True)]
    reduce_sum x2 -> x0, other arithmetic: 5.17 us -> none  [the longest x1 5.12 us: on_device(): proto_sq = jnp.sum(jnp.square(full.astype(jnp.float32)), axis=1)]
  transfers between devices with their start and end apart: 4 -> 0, of which waited for: 4 -> 0; matrix products, arithmetic and copies ran while one was open for 1% -> 0% of each run, Pallas kernels for 0% -> 0%
where the time goes in v1:
time: 144 us
  Pallas kernels  132 us (92%)
  other arithmetic  8.94 us (6%)
  local copies, waits for them, and re-layouts  2.81 us (2%)
    pallas_call x1, Pallas kernels, with_kernel(): pl.pallas_call(functools.partial(kernel, n_rows, n_protos, masked, protos...  132 us
    convert_element_type x1, other arithmetic, with_kernel(): (row_scale * weights * cs[ITERS - 1].reshape(1, total)).astype(jnp.bfloat16)  8.84 us

profile of v1, /device:TPU:0, one launch (start us, length us, event | category | flops | bytes accessed | tf_op | source)
XLA Modules:
  0.0 143.7 jit_solution(787214922589666466)
XLA Ops:
  0.0 0.8 copy.4.index_ref
  0.8 0.0 copy-start
  0.8 1.2 copy-done
  2.0 0.0 copy-start.1
  2.0 0.8 copy-done.1
  2.8 131.9 %shard_map.37 = (f32[192,16384]{1,0:T(8,128)}, f32[256,128]{1,0:T(8,128)S(1)}, f32[3,8,1,2048]{3,2,1,0:T(1,128)S(1)}) custom-call(bf16[64,384]{1,0:T(8,128)(2,1)S(1)} %bitcast.5, bf16[32,16384]{1,0:T(8,128)(2,1)S(1)} %bitcast.4, s32[192,1]{1,0:T(8,128)S(1)} %copy.4.index_ref), custom_call_target="tpu_custom_call" | custom-call | tf_op jit(solution)/shard_map/pallas_call | solution.py:337
  134.8 0.1 multiply_reduce_fusion
  134.9 8.8 %multiply_convert_fusion = bf16[192,16384]{1,0:T(8,128)(2,1)} fusion(f32[192,16384]{1,0:T(8,128)} %get-tuple-element.9, f32[16384]{0:T(1024)S(1)} %bitcast.6, f32[192]{0:T(256)S(1)} %multiply_reduce_fusion), kind=kLoop, calls=%fused_computation | loop fusion | flops 9437184 | bytes 18940672 | tf_op jit(solution)/shard_map/convert_element_type | solution.py:375
  (1 shorter events, 0.0 us)
Async XLA Ops:
  0.8 1.2 copy-start
  2.0 0.8 copy-start.1

commit v2 on v1

--- a/solution.py
+++ b/solution.py
@@ -14,13 +14,14 @@
 EPS = 1e-06
 UP, DOWN, ACROSS = 0, 1, 2
 LEAD = 2
+SPLIT = 1
 
 
 def kernel(
     n_rows, n_protos, masked, protos_all,
-    feat_ref, proto_ref, index_ref, weights_ref, rs_ref, cs_ref,
-    feat_full, full, chosen, feat_scale, weights, acc, parts, masses, row_out, row_in,
-    feat_send, feat_recv, own_sem, send, recv, out_sem,
+    feat_ref, proto_ref, index_ref, weights, rs_ref, cs_ref,
+    feat_full, index, onehot, full, chosen, feat_scale, acc, parts, masses, row_out, row_in,
+    feat_send, feat_recv, in_sem, own_sem, send, recv,
     mass_send, mass_recv, scale_send, scale_recv, row_send, row_recv,
 ):
     r, p = lax.axis_index("rows"), lax.axis_index("protos")
@@ -29,9 +30,11 @@
     other = 1 - y
     dim, total = proto_ref.shape
     width = total // n_rows
-    rows = index_ref.shape[0]
+    chunks = n_rows * SPLIT
+    span = total // chunks
+    rows = weights.shape[0]
     fdim = feat_ref.shape[0]
-    tile = min(512, width)
+    tile = min(512, span)
     tiles = width // tile
     mesh_id = pl.DeviceIdType.MESH
 
@@ -47,17 +50,16 @@
     pl.semaphore_wait(barrier, n_rows + n_protos - 2)
 
     def where(src, c):
-        return (
-            pl.ds(pl.multiple_of(src * dim, dim), dim),
-            pl.ds(pl.multiple_of(c * width, width), width),
-        )
+        return full.at[c, pl.ds(pl.multiple_of(src * dim, dim), dim)]
+
+    def given(c):
+        return proto_ref.at[:, pl.ds(pl.multiple_of(c * span, span), span)]
 
     def block_copy(way, src, c, own=False):
-        spot = where(src, c)
         target = {UP: r + 2, DOWN: r - 2, ACROSS: z * 2 + other}[way]
         return pltpu.make_async_remote_copy(
-            src_ref=proto_ref.at[:, spot[1]] if own else full.at[spot],
-            dst_ref=full.at[spot],
+            src_ref=given(c) if own else where(src, c),
+            dst_ref=where(src, c),
             send_sem=send.at[way, src, c],
             recv_sem=recv.at[src, c],
             device_id={"rows": target},
@@ -65,9 +67,7 @@
         )
 
     def own_copy(c):
-        return pltpu.make_async_copy(
-            proto_ref.at[:, where(r, c)[1]], full.at[where(r, c)], own_sem.at[c]
-        )
+        return pltpu.make_async_copy(given(c), where(r, c), own_sem.at[c])
 
     def send_own(c):
         @pl.when(z < nz - 1)
@@ -92,20 +92,25 @@
             device_id_type=mesh_id,
         )
 
+    index_in = pltpu.make_async_copy(index_ref, index, in_sem.at[0])
+    feat_in = pltpu.make_async_copy(
+        feat_ref, feat_full.at[pl.ds(pl.multiple_of(p * fdim, fdim), fdim)], in_sem.at[1]
+    )
     for step in range(1, n_protos):
         feat_copy(step).start()
     for c in range(LEAD):
         send_own(c)
-    feat_full[pl.ds(pl.multiple_of(p * fdim, fdim), fdim), :] = feat_ref[...]
+    index_in.start()
+    feat_in.start()
+    onehot[...] = jnp.zeros_like(onehot)
+    index_in.wait()
+    hits = lax.broadcasted_iota(jnp.int32, (onehot.shape[0], rows), 0) == index[...]
+    onehot[:, :rows] = hits.astype(jnp.float32).astype(jnp.bfloat16)
+    feat_in.wait()
     for step in range(1, n_protos):
         feat_copy(step).wait()
-    onehot = lax.broadcasted_iota(jnp.int32, (rows, feat_ref.shape[1]), 1) == index_ref[...]
-    picked = lax.dot_general(
-        onehot.astype(jnp.float32).astype(jnp.bfloat16),
-        feat_full[...],
-        (((1,), (1,)), ((), ())),
-        preferred_element_type=jnp.float32,
-    )
+    picked = jnp.dot(feat_full[...], onehot[...], preferred_element_type=jnp.float32)
+    picked = picked.T[:rows]
     chosen[...] = picked.astype(jnp.bfloat16)
     scale = lax.rsqrt(jnp.sum(picked * picked, axis=1, keepdims=True) + EPS)
     feat_scale[...] = jnp.broadcast_to(scale * (1.0 / TEMP), feat_scale.shape)
@@ -130,24 +135,20 @@
         def _():
             mass_copy(it, c, r).start()
 
-    def out_copy(c):
-        columns = where(r, c)[1]
-        return pltpu.make_async_copy(
-            weights.at[:, columns], weights_ref.at[:, columns], out_sem.at[c]
-        )
-
     def make_weights(c):
-        for t in range(tiles):
-            columns = pl.ds(pl.multiple_of(c * width + t * tile, tile), tile)
-            block = full[:, columns]
+        for t in range(span // tile):
+            columns = pl.ds(pl.multiple_of(c * span + t * tile, tile), tile)
+            within = pl.ds(pl.multiple_of(lax.rem(c, SPLIT) * span + t * tile, tile), tile)
+            block = full[c, :, t * tile:(t + 1) * tile]
             wide = block.astype(jnp.float32)
             proto_scale = lax.rsqrt(jnp.sum(wide * wide, axis=0, keepdims=True) + EPS)
             raw = jnp.dot(chosen[...], block, preferred_element_type=jnp.float32)
             value = jnp.exp(raw * feat_scale[:, :1] * proto_scale)
             weights[:, columns] = value
-            parts[0, c, :, t * tile:(t + 1) * tile] = jnp.sum(value, axis=0, keepdims=True)
-
-    middle = n_rows // 2
+            parts[0, c // SPLIT, :, within] = jnp.sum(value, axis=0, keepdims=True)
+
+    def early(c):
+        return c == 4
 
     def line(c, d):
         for way, ahead, more, there in (
@@ -164,7 +165,7 @@
                 def _():
                     block_copy(way, src, c).start()
 
-                @pl.when(c != middle)
+                @pl.when(jnp.logical_not(early(c)))
                 def _():
                     block_copy(ACROSS, src, c).start()
 
@@ -179,7 +180,7 @@
             def _():
                 block_copy(ACROSS, src, c).wait_recv()
 
-                @pl.when(jnp.logical_and(more, c == middle))
+                @pl.when(jnp.logical_and(more, early(c)))
                 def _():
                     block_copy(way, src, c).start()
 
@@ -187,44 +188,56 @@
         src = z * 2 + other
         block_copy(ACROSS, src, c).wait_recv()
 
-        @pl.when(jnp.logical_and(z < nz - 1, c == middle))
+        @pl.when(jnp.logical_and(z < nz - 1, early(c)))
         def _():
             block_copy(UP, src, c).start()
 
-        @pl.when(jnp.logical_and(z > 0, c == middle))
+        @pl.when(jnp.logical_and(z > 0, early(c)))
         def _():
             block_copy(DOWN, src, c).start()
 
     def step_of(i, carry):
-        @pl.when(i + LEAD < n_rows)
+        @pl.when(i + LEAD < chunks)
         def _():
             send_own(i + LEAD)
 
-        @pl.when(i < n_rows)
+        @pl.when(i < chunks)
         def _():
             beside(i)
 
         for d in range(1, nz):
             c = i - (d - 1)
 
-            @pl.when(jnp.logical_and(c >= 0, c < n_rows))
+            @pl.when(jnp.logical_and(c >= 0, c < chunks))
             def _():
                 line(c, d)
 
+        for d in range(1, nz):
+            c = i - d
+
+            @pl.when(jnp.logical_and(jnp.logical_and(c >= 0, c < chunks), early(c)))
+            def _():
+                far_line(c, d)
+
         last = i - (nz - 1)
 
-        @pl.when(last >= 0)
+        @pl.when(jnp.logical_and(last >= 0, jnp.logical_not(early(last))))
         def _():
             for d in range(1, nz):
                 far_line(last, d)
+
+        @pl.when(last >= 0)
+        def _():
             own_copy(last).wait()
             make_weights(last)
-            out_copy(last).start()
-            give_mass(0, last)
+
+            @pl.when(lax.rem(last, SPLIT) == SPLIT - 1)
+            def _():
+                give_mass(0, last // SPLIT)
 
         return carry
 
-    lax.fori_loop(0, n_rows + nz - 1, step_of, 0)
+    lax.fori_loop(0, chunks + nz - 1, step_of, 0)
 
     def scale_copy(it, c, step):
         return pltpu.make_async_remote_copy(
@@ -298,13 +311,12 @@
             row_copy(it, step).wait_send()
 
     def drain(c, carry):
-        out_copy(c).wait()
         for src_z in range(nz):
             for src_y in range(2):
                 src = src_z * 2 + src_y
                 on_line = src_y == y
                 beside_me = jnp.logical_and(src_y != y, src_z == z)
-                moved = jnp.logical_or(on_line, c == middle)
+                moved = jnp.logical_or(on_line, early(c))
 
                 @pl.when(jnp.logical_and(moved, jnp.logical_and(src_z <= z, z < nz - 1)))
                 def _():
@@ -314,13 +326,41 @@
                 def _():
                     block_copy(DOWN, src, c).wait_send()
 
-                @pl.when(jnp.logical_and(on_line, jnp.logical_or(src_z == z, c != middle)))
+                @pl.when(jnp.logical_and(on_line, jnp.logical_or(src_z == z, jnp.logical_not(early(c)))))
                 def _():
                     block_copy(ACROSS, src, c).wait_send()
 
         return carry
 
-    lax.fori_loop(0, n_rows, drain, 0)
+    lax.fori_loop(0, chunks, drain, 0)
+
+
+def finish(factor, weights, rs_ref, cs_ref, out_ref, buffer, out_sem):
+    rows, total = weights.shape
+    count, width = cs_ref.shape[0], cs_ref.shape[2]
+    slots = buffer.shape[0]
+
+    def out_copy(c):
+        columns = pl.ds(pl.multiple_of(c * width, width), width)
+        slot = lax.rem(c, slots)
+        return pltpu.make_async_copy(buffer.at[slot], out_ref.at[:, columns], out_sem.at[slot])
+
+    def block(c, carry):
+        @pl.when(c >= slots)
+        def _():
+            out_copy(c - slots).wait()
+
+        for t in range(width // 128):
+            columns = pl.ds(pl.multiple_of(c * width + t * 128, 128), 128)
+            col_scale = cs_ref[c, :, t * 128:(t + 1) * 128]
+            value = (factor * rs_ref[:rows, :]) * weights[:, columns] * col_scale
+            buffer[lax.rem(c, slots), :, t * 128:(t + 1) * 128] = value.astype(jnp.bfloat16)
+        out_copy(c).start()
+        return carry
+
+    lax.fori_loop(0, count, block, 0)
+    for c in range(max(0, count - slots), count):
+        out_copy(c).wait()
 
 
 def with_kernel(n_rows, n_protos, features, prototypes, masked_index):
@@ -341,14 +381,15 @@
             jax.ShapeDtypeStruct((padded, 128), f32),
             jax.ShapeDtypeStruct((ITERS, n_rows, 1, width), f32),
         ),
-        in_specs=[vmem, anywhere, vmem],
-        out_specs=(anywhere, vmem, vmem),
+        in_specs=[pl.BlockSpec(memory_space=pltpu.HBM)] * 3,
+        out_specs=(vmem, vmem, vmem),
         scratch_shapes=[
             pltpu.VMEM((fdim * n_protos, patches), bf16),
-            pltpu.VMEM((dim * n_rows, total), bf16),
+            pltpu.VMEM((1, rows), jnp.int32),
+            pltpu.VMEM((patches, padded), bf16),
+            pltpu.VMEM((n_rows * SPLIT, dim * n_rows, width // SPLIT), bf16),
             pltpu.VMEM((rows, fdim * n_protos), bf16),
             pltpu.VMEM((rows, 128), f32),
-            pltpu.VMEM((rows, total), f32),
             pltpu.VMEM((padded, 128), f32),
             pltpu.VMEM((ITERS, n_rows, 1, width), f32),
             pltpu.VMEM((ITERS, n_rows, 1, width), f32),
@@ -356,10 +397,10 @@
             pltpu.VMEM((ITERS, n_protos, 1, padded), f32),
             dma((n_protos,)),
             dma((n_protos,)),
-            dma((n_rows,)),
-            dma((3, n_rows, n_rows)),
-            dma((n_rows, n_rows)),
-            dma((n_rows,)),
+            dma((2,)),
+            dma((n_rows * SPLIT,)),
+            dma((3, n_rows, n_rows * SPLIT)),
+            dma((n_rows, n_rows * SPLIT)),
             dma((ITERS, n_rows)),
             dma((ITERS, n_rows)),
             dma((ITERS, n_rows)),
@@ -368,11 +409,17 @@
             dma((ITERS, n_protos)),
         ],
         compiler_params=pltpu.CompilerParams(
-            collective_id=0, has_side_effects=True, vmem_limit_bytes=48 * 1024 * 1024
+            collective_id=0, has_side_effects=True, vmem_limit_bytes=20 * 1024 * 1024
         ),
-    )(features.T, prototypes.T, masked_index[:, None])
-    row_scale = (protos_all * masked) * rs[:rows, :1]
-    return (row_scale * weights * cs[ITERS - 1].reshape(1, total)).astype(jnp.bfloat16)
+    )(features.T, prototypes.T, masked_index[None, :])
+    return pl.pallas_call(
+        functools.partial(finish, protos_all * masked),
+        out_shape=jax.ShapeDtypeStruct((rows, total), bf16),
+        in_specs=[vmem, vmem, vmem],
+        out_specs=anywhere,
+        scratch_shapes=[pltpu.VMEM((4, rows, width), bf16), dma((4,))],
+        compiler_params=pltpu.CompilerParams(vmem_limit_bytes=20 * 1024 * 1024),
+    )(weights, rs, cs[ITERS - 1])
 
 
 def with_collectives(features, prototypes, masked_index):
@@ -409,7 +456,7 @@
             and n_rows <= 8
             and prototypes.shape[1] % 16 == 0
             and features.shape[1] % 16 == 0
-            and prototypes.shape[0] % (n_rows * 128) == 0
+            and prototypes.shape[0] % (n_rows * SPLIT * 128) == 0
         )
         if fits:
             return with_kernel(n_rows, n_protos, features, prototypes, masked_index)

time: 144 us -> 136 us (0.944)
  other arithmetic: 8.94 us -> 0 us
    convert_element_type x1 -> x0, other arithmetic: 8.84 us -> none  [with_kernel(): (row_scale * weights * cs[ITERS - 1].reshape(1, total)).astype(jnp.bfloat16)]
    pallas_call x0 -> x1, Pallas kernels: none -> 3.08 us  [with_kernel(): pl.pallas_call(functools.partial(finish, protos_all * masked), out_shape=...]
    pallas_call x1, Pallas kernels: 132 us -> 130 us  [with_kernel(): pl.pallas_call(functools.partial(kernel, n_rows, n_protos, masked, protos...]
where the time goes in v2:
time: 136 us
  Pallas kernels  133 us (98%)
  local copies, waits for them, and re-layouts  2.71 us (2%)
    pallas_call x1, Pallas kernels, with_kernel(): pl.pallas_call(functools.partial(kernel, n_rows, n_protos, masked, protos...  130 us
    pallas_call x1, Pallas kernels, with_kernel(): pl.pallas_call(functools.partial(finish, protos_all * masked), out_shape=...  3.08 us

profile of v2, /device:TPU:0, one launch (start us, length us, event | category | flops | bytes accessed | tf_op | source)
XLA Modules:
  0.0 136.0 jit_solution(6021169992642667616)
XLA Ops:
  0.0 0.0 copy-start
  0.0 1.2 copy-done
  1.2 0.0 copy-start.1
  1.2 0.8 copy-done.1
  2.0 0.0 copy-start.2
  2.0 0.7 copy-done.2
  2.7 130.2 %shard_map.37 = (f32[192,16384]{1,0:T(8,128)S(1)}, f32[256,128]{1,0:T(8,128)S(1)}, f32[3,8,1,2048]{3,2,1,0:T(1,128)S(1)}) custom-call(bf16[64,384]{1,0:T(8,128)(2,1)S(1)} %bitcast.6, bf16[32,16384]{1,0:T(8,128)(2,1)S(1)} %bitcast.5, s32[1,192]{1,0:T(1,128)S(1)} %bitcast.7), custom_call_target="tpu_custom_call" | custom-call | tf_op jit(solution)/shard_map/pallas_call | solution.py:377
  133.0 3.1 %shard_map.38 = bf16[192,16384]{1,0:T(8,128)(2,1)} custom-call(f32[192,16384]{1,0:T(8,128)S(1)} %get-tuple-element.8.weights, f32[256,128]{1,0:T(8,128)S(1)} %get-tuple-element.9.rs_ref, f32[8,1,2048]{2,1,0:T(1,128)S(1)} %slice_bitcast_fusion.cs_ref), custom_call_target="tpu_custom_call" | custom-call | tf_op jit(solution)/shard_map/pallas_call | solution.py:415
  (1 shorter events, 0.0 us)
Async XLA Ops:
  0.0 1.2 copy-start
  1.2 0.8 copy-start.1
  2.0 0.7 copy-start.2
